TPU v7x, 128 devices: a whole 4x4x4 slice. The times are simulated.
128 devices in a mesh: replica: 4 (over x), data: 32 (over z, y, core).
Axes of the slice: x: 4, y: 4, z: 4, core: 2. Of those that a mesh axis runs over, the one named last changes fastest.
Arguments:
- img_x: bfloat16 [32768, 1024], P(('replica', 'data'))
- txt_x: bfloat16 [32768, 1024], P(('replica', 'data'))
- w_img: bfloat16 [1024, 1024], replicated
- w_txt: bfloat16 [1024, 1024], replicated
- log_temp: float32 [1], replicated
- logit_bias: float32 [1], replicated
Outputs:
- output 1: float32 [1], replicated
- output 2: float32 [1], replicated
- output 3: float32 [1], replicated
- output 4: float32 [1024, 1024], replicated
- output 5: float32 [1024, 1024], replicated
All inputs are finite; a program needn't handle non-finite values.
Results may differ from a plain program's by a relative error of at most 0.001.
Values are sent between devices in bfloat16 or wider.
A program may use at most 1 GiB of HBM per device.

v0:
```python
import jax
import jax.numpy as jnp
from jax import lax
from jax.sharding import PartitionSpec as P


def normalize(raw):
    return raw * lax.rsqrt(jnp.sum(raw * raw, axis=-1, keepdims=True))


def embed_rows(feat_x, w_proj):
    raw_emb = jnp.dot(feat_x, w_proj, preferred_element_type=jnp.float32)
    unit_emb, pull_back = jax.vjp(normalize, raw_emb)
    return unit_emb.astype(jnp.bfloat16), pull_back


def tile_terms(img_emb, txt_blk, labels, temp_scale, bias_val, total_rows):
    sim_tile = jnp.einsum("id,jd->ij", img_emb, txt_blk, preferred_element_type=jnp.float32)
    logits = temp_scale * sim_tile + bias_val
    loss_part = -jnp.sum(jax.nn.log_sigmoid(labels * logits))
    grad_tile = -labels * jax.nn.sigmoid(-labels * logits) / total_rows
    grad_b = grad_tile.astype(jnp.bfloat16)
    d_img = jnp.dot(grad_b, txt_blk, preferred_element_type=jnp.float32)
    d_txt = jnp.einsum("ij,id->jd", grad_b, img_emb, preferred_element_type=jnp.float32)
    return loss_part, jnp.sum(grad_tile * sim_tile), jnp.sum(grad_tile), d_img, d_txt


def solution(mesh):
    rep_count = mesh.shape["replica"]
    data_count = mesh.shape["data"]
    dev_count = rep_count * data_count
    batch_axes = ("replica", "data")
    next_perm = [(k, (k + 1) % dev_count) for k in range(dev_count)]

    def local_fn(img_x, txt_x, w_img, w_txt, log_temp, logit_bias):
        local_rows = img_x.shape[0]
        total_rows = local_rows * dev_count
        img_emb, img_pull = embed_rows(img_x, w_img)
        txt_emb, txt_pull = embed_rows(txt_x, w_txt)
        temp_scale = jnp.exp(log_temp[0])
        bias_val = logit_bias[0]
        row_ids = lax.broadcasted_iota(jnp.int32, (local_rows, 1), 0)
        col_ids = lax.broadcasted_iota(jnp.int32, (1, local_rows), 1)
        diag_labels = jnp.where(row_ids == col_ids, 1.0, -1.0)
        first = tile_terms(img_emb, txt_emb, diag_labels, temp_scale, bias_val, total_rows)

        def hop(step, state):
            txt_blk, d_txt_acc, d_img_acc, loss_acc, temp_acc, bias_acc = state
            txt_blk = lax.ppermute(txt_blk, batch_axes, next_perm)
            d_txt_acc = lax.ppermute(d_txt_acc, batch_axes, next_perm)
            loss_part, temp_part, bias_part, d_img_part, d_txt_part = tile_terms(img_emb, txt_blk, -1.0, temp_scale, bias_val, total_rows)
            return (txt_blk, d_txt_acc + d_txt_part, d_img_acc + d_img_part, loss_acc + loss_part, temp_acc + temp_part, bias_acc + bias_part)

        init_state = (txt_emb, first[4], first[3], first[0], first[1], first[2])
        final_state = lax.fori_loop(1, dev_count, hop, init_state)
        d_txt_home = lax.ppermute(final_state[1], batch_axes, next_perm)
        d_img_raw = img_pull(temp_scale * final_state[2])[0].astype(jnp.bfloat16)
        d_txt_raw = txt_pull(temp_scale * d_txt_home)[0].astype(jnp.bfloat16)
        d_w_img = jnp.einsum("nf,nd->fd", img_x, d_img_raw, preferred_element_type=jnp.float32)
        d_w_txt = jnp.einsum("nf,nd->fd", txt_x, d_txt_raw, preferred_element_type=jnp.float32)
        loss_total, temp_total, bias_total, d_w_img, d_w_txt = lax.psum((final_state[3], final_state[4], final_state[5], d_w_img, d_w_txt), batch_axes)
        loss_out = jnp.reshape(loss_total / total_rows, (1,))
        d_log_temp = jnp.reshape(temp_scale * temp_total, (1,))
        d_logit_bias = jnp.reshape(bias_total, (1,))
        return loss_out, d_log_temp, d_logit_bias, d_w_img, d_w_txt

    batch_spec = P(batch_axes, None)
    return jax.shard_map(local_fn, mesh=mesh, in_specs=(batch_spec, batch_spec, P(), P(), P(), P()), out_specs=(P(), P(), P(), P(), P()), check_vma=False)
```

profile of v0, /device:TPU:1, one launch (start us, length us, event | category | flops | bytes accessed | tf_op | source)
XLA Modules:
  0.0 4029.8 jit_solution(10743447774882757271)
XLA Ops:
  17.6 3800.8 %while.20 = (s32[]{:T(128)}, bf16[256,1024]{1,0:T(8,128)(2,1)}, f32[256,1024]{1,0:T(8,128)}, f32[256,1024]{1,0:T(8,128)}, f32[]{:T(128)}, /*index=5*/f32[]{:T(12...) while((s32[]{:T(128)}, bf16[256,1024]{1,0:T(8,128)(2,1)}, ...), condition=%wide.region_9.10_spmd, body=%wide.region_5.9_spmd.sunk | while | flops 405274624 | bytes 14418181 | solution.py:55
  155.8 15.8 collective-permute-done
  185.8 15.8 collective-permute-done
  215.9 15.8 collective-permute-done
  245.9 15.8 collective-permute-done
  275.9 15.8 collective-permute-done
  305.9 15.8 collective-permute-done
  336.0 15.8 collective-permute-done
  366.0 15.8 collective-permute-done
  396.0 15.8 collective-permute-done
  426.0 15.8 collective-permute-done
  456.0 15.8 collective-permute-done
  486.1 15.8 collective-permute-done
  516.1 15.8 collective-permute-done
  546.1 15.8 collective-permute-done
  576.1 15.8 collective-permute-done
  606.1 15.8 collective-permute-done
  636.2 15.8 collective-permute-done
  666.2 15.8 collective-permute-done
  696.2 15.8 collective-permute-done
  726.2 15.8 collective-permute-done
  756.2 15.8 collective-permute-done
  786.3 15.8 collective-permute-done
  816.3 15.8 collective-permute-done
  846.3 15.8 collective-permute-done
  876.3 15.8 collective-permute-done
  906.4 15.8 collective-permute-done
  936.4 15.8 collective-permute-done
  966.4 15.8 collective-permute-done
  996.4 15.8 collective-permute-done
  1026.4 15.8 collective-permute-done
  1056.5 15.8 collective-permute-done
  1266.6 15.8 collective-permute-done
  1506.8 15.8 collective-permute-done
  1596.8 15.8 collective-permute-done
  1837.0 15.8 collective-permute-done
  2077.2 15.8 collective-permute-done
  2167.2 15.8 collective-permute-done
  2407.4 15.8 collective-permute-done
  2647.6 15.8 collective-permute-done
  2737.6 15.8 collective-permute-done
  2977.8 15.8 collective-permute-done
  3218.0 15.8 collective-permute-done
  3308.0 15.8 collective-permute-done
  3548.2 15.8 collective-permute-done
  3788.4 15.8 collective-permute-done
  3838.1 79.9 %all-reduce = (f32[]{:T(128)}, f32[]{:T(128)}, f32[1]{0:T(128)}) all-reduce(f32[]{:T(128)} %get-tuple-element.61, f32[]{:T(128)} %get-tuple-element.62, f32[1]{0:T(128)} %bitcast.4), channel_id=1, replica_groups=mesh['replica'=4,'data'=32] {'replica','data'}, use_global_device_ids=true, to_apply=%region_10.11 | all-reduce | flops 3 | bytes 24 | tf_op jit(solution)/shard_map/psum | solution.py:61
  3919.3 90.8 %all-reduce.4.cloned.1.call-done = (f32[1024,1024]{0,1:T(8,128)}, f32[1024,1024]{0,1:T(8,128)}) async-done(((f32[1024,1024]{0,1:T(8,128)}, f32[1024,1024]{0,1:T(8,128)}), (f32[1024,1024]{0,1:T(8,128)}, f32[1024,1024]{0,1:T(8,128)})) %all-reduce.4.cloned.1.call-update) | async-done | bytes 8388624 | tf_op jit(solution)/shard_map/psum | solution.py:61
  (1003 shorter events, 2456.2 us)
Async XLA Ops:
  7.2 4002.8 %all-reduce.4.cloned.1.call-start = ((), (), s32[]{:S(2)}) async-start(), calls=%async_computation | async-start | bytes 16777216 | tf_op jit(solution)/shard_map/psum | solution.py:61
  155.8 25.3 collective-permute-start.1
  185.8 25.3 collective-permute-start.1
  215.9 25.3 collective-permute-start.1
  245.9 25.3 collective-permute-start.1
  305.9 25.3 collective-permute-start.1
  396.0 25.3 collective-permute-start.1
  456.0 25.3 collective-permute-start.1
  546.1 25.3 collective-permute-start.1
  636.2 25.3 collective-permute-start.1
  726.2 25.3 collective-permute-start.1
  786.3 25.3 collective-permute-start.1
  876.3 25.3 collective-permute-start.1
  966.4 25.3 collective-permute-start.1
  1026.4 25.3 collective-permute-start.1
  1116.5 25.3 collective-permute-start.1
  1206.6 25.3 collective-permute-start.1
  1296.6 25.3 collective-permute-start.1
  1356.7 25.3 collective-permute-start.1
  1446.7 25.3 collective-permute-start.1
  1536.8 25.3 collective-permute-start.1
  1596.8 25.3 collective-permute-start.1
  1686.9 25.3 collective-permute-start.1
  1777.0 25.3 collective-permute-start.1
  1867.0 25.3 collective-permute-start.1
  1927.1 25.3 collective-permute-start.1
  2017.1 25.3 collective-permute-start.1
  2107.2 25.3 collective-permute-start.1
  2167.2 25.3 collective-permute-start.1
  2257.3 25.3 collective-permute-start.1
  2347.4 25.3 collective-permute-start.1
  2437.4 25.3 collective-permute-start.1
  2497.5 25.3 collective-permute-start.1
  2587.5 25.3 collective-permute-start.1
  2677.6 25.3 collective-permute-start.1
  2737.6 25.3 collective-permute-start.1
  2827.7 25.3 collective-permute-start.1
  2917.8 25.3 collective-permute-start.1
  3007.8 25.3 collective-permute-start.1
  3067.9 25.3 collective-permute-start.1
  3157.9 25.3 collective-permute-start.1
  3248.0 25.3 collective-permute-start.1
  3308.0 25.3 collective-permute-start.1
  3398.1 25.3 collective-permute-start.1
  3488.2 25.3 collective-permute-start.1
  3578.2 25.3 collective-permute-start.1
  3638.3 25.3 collective-permute-start.1
  3728.3 25.3 collective-permute-start.1
  (214 other events, 4049.2 us)
Sparse Core Ops, SparseCore 0:
  3838.2 171.7 all-reduce.3
where the time goes:
time: 4050 us; the launch traced here: 4030 us
  waiting for transfers between devices  2080 us (51%)
  matrix products  1050 us (26%)
  loops' own time  675 us (17%)
  local copies, waits for them, and re-layouts  112 us (3%)
  blocking collectives  79.9 us (2%)
    ppermute x127, waiting for transfers between devices, hop(): txt_blk = lax.ppermute(txt_blk, batch_axes, next_perm)  1980 us
    another operation x1, loops' own time, local_fn(): final_state = lax.fori_loop(1, dev_count, hop, init_state)  675 us
    dot_general x128, matrix products, tile_terms(): jnp.einsum('ij,id->jd', grad_b, img_emb, preferred_element_type=jnp.float32)  408 us
    dot_general x128, matrix products, tile_terms(): d_img = jnp.dot(grad_b, txt_blk, preferred_element_type=jnp.float32)  405 us
    dot_general x128, matrix products, tile_terms(): jnp.einsum('id,jd->ij', img_emb, txt_blk, preferred_element_type=jnp.floa...  226 us
    while x127, local copies, waits for them, and re-layouts  101 us
    psum x1, waiting for transfers between devices, local_fn(): lax.psum((final_state[3], final_state[4], final_state[5], d_w_img, d_w_tx...  90.8 us
  transfers between devices with their start and end apart: 256, of which 131 were waited for; matrix products, arithmetic and copies ran while one was open for 18% of the time, Pallas kernels for 0%

commit v1 on v0

v1 whole, which is shorter than its diff:
```python
import functools

import jax
import jax.numpy as jnp
from jax import lax
from jax.experimental import pallas as pl
from jax.experimental.pallas import tpu as pltpu
from jax.sharding import PartitionSpec as P

LOG2E = 1.4426950408889634
LN2 = 0.6931471805599453
MESH = pl.DeviceIdType.MESH
VMEM_BYTES = 67043328
F32 = jnp.float32
BF16 = jnp.bfloat16
NN = (((1,), (0,)), ((), ()))
NT = (((1,), (1,)), ((), ()))
TN = (((0,), (0,)), ((), ()))
BOTH = range(2)
DIMS = range(3)


def digits(word):
    return tuple(int(c, 36) for c in word)


def dot(a, b, dims):
    return lax.dot_general(a, b, dims, preferred_element_type=F32)


def position():
    d = lax.axis_index("data")
    chip = [lax.axis_index("replica"), lax.rem(lax.div(d, 2), 4), lax.div(d, 8)]
    return chip, lax.rem(d, 2)


def device(chip, core):
    return (chip[0], (chip[2] * 4 + chip[1]) * 2 + core)


def partner(v, kind):
    t = v + kind
    return lax.rem(t + 5 - 2 * lax.rem(t, 2) - kind, 4)


def neighbour(chip, core, dim, kind):
    return device([partner(v, kind) if i == dim else v for i, v in enumerate(chip)], core)


def copy_to(src, dst, send, recv, dev):
    return pltpu.make_async_remote_copy(src, dst, send, recv, device_id=dev, device_id_type=MESH)


def parts_of(h):
    a = h // 24 * 8 if h % 24 == 0 else (h // 3 + 7) // 8 * 8
    b = (h - a) // 16 * 8
    return [(0, a), (a, b), (a + b, h - a - b)]


EARLY = digits("0124")
LATE = digits("356")


def score_kernel(rows, width, sc, x_img, x_txt, w_img, w_txt, du_img, du_txt, sums,
                 raw, xb, ie, te, g, sbuf, rbuf, tmp, far, near, s0, s1, fin, acc,
                 load_sem, ag_send, ag_recv, tx_send, tx_recv, rs_send, rs_recv, dt_send, dt_recv, credit):
    h = rows // 2
    parts = parts_of(h)
    chip, core = position()
    other = device(chip, 1 - core)
    nbr = [[neighbour(chip, core, dim, kind) for dim in DIMS] for kind in BOTH]

    loads = []
    for i, (src, dst) in enumerate(((x_img, xb.at[0]), (x_txt, xb.at[1]),
                                    (w_img, sbuf.at[0, 0:width]), (w_txt, sbuf.at[1, 0:width]))):
        loads.append(pltpu.make_async_copy(src, dst, load_sem.at[i]))
        loads[-1].start()
    barrier = pltpu.get_barrier_semaphore()
    for dev in (*nbr[0], *nbr[1], other):
        pl.semaphore_signal(barrier, inc=1, device_id=dev, device_id_type=MESH)

    def irow(s, hh):
        if s in EARLY:
            return hh * 4 * h + EARLY.index(s) * h
        return (8 + hh * 3 + LATE.index(s)) * h if s in LATE else (14 + hh) * h

    def trow(s, hh, c=0):
        if s in EARLY:
            return (hh * 8 + c * 4 + EARLY.index(s)) * h
        return (16 + hh * 6 + c * 3 + LATE.index(s)) * h if s in LATE else (28 + c * 2 + hh) * h

    emb = (ie, te)
    row = (irow, trow)

    for kind in BOTH:
        loads[kind].wait()
        loads[2 + kind].wait()
        step = min(256, width)

        def project(j, _, kind=kind):
            cols = pl.ds(pl.multiple_of(j * step, step), step)
            raw[kind, :, cols] = dot(xb[kind], sbuf[kind, 0:width, cols], NN)
            return 0

        lax.fori_loop(0, width // step, project, 0)
        for hh in BOTH:
            u = raw[kind, hh * h:(hh + 1) * h, :]
            unit = u * lax.rsqrt(jnp.sum(u * u, axis=1, keepdims=True))
            emb[kind][row[kind](0, hh):row[kind](0, hh) + h, :] = unit.astype(BF16)

    ways = [digits(w) for w in "0023 0146 0215 1045 1113 1226".split()]
    whole = (0, h)
    ag = [(dim, (0, hh), (1 << dim, hh), whole) for hh in BOTH for dim in DIMS]
    ag += [(dim, (s, hh), (t, hh), whole) for hh, dim, s, t in ways]
    ag += [(dim, (7 ^ (1 << dim), hh), (7, hh), parts[dim]) for hh in BOTH for dim in DIMS]

    def ag_copy(kind, m):
        dim, (s, hs), (t, ht), (at, n) = ag[m]
        src = row[kind](s, hs) + at
        dst = row[kind](t, ht) + at
        return copy_to(emb[kind].at[src:src + n], emb[kind].at[dst:dst + n],
                       ag_send.at[kind, m], ag_recv.at[kind, m], nbr[kind][dim])

    def ag_start(k):
        for dim in DIMS:
            for kind in BOTH:
                ag_copy(kind, k * 3 + dim).start()

    def ag_wait(*ks):
        for k in ks:
            for dim in DIMS:
                for kind in BOTH:
                    ag_copy(kind, k * 3 + dim).wait_recv()

    share = [digits(w) for w in "014 81c 135 93d g3j m3p s2u".split()]

    def tx_copy(i):
        src, n, dst = (v * h for v in share[i])
        return copy_to(te.at[src:src + n], te.at[dst:dst + n], tx_send.at[i], tx_recv.at[i], other)

    k1, k0 = sc[0], sc[1]
    acc[:] = jnp.zeros_like(acc)

    def fold(x):
        return jnp.sum(x.reshape(x.shape[0] // 8, 8, x.shape[1]), axis=0)

    def entries(s, r0, c0, diagonal=False):
        tm, tn = s.shape
        z = s * k1 + k0
        if diagonal:
            i = lax.broadcasted_iota(jnp.int32, (tm, tn), 0)
            j = lax.broadcasted_iota(jnp.int32, (tm, tn), 1)
            eye = (i == j) & (i < h)
            z = jnp.where(eye, -z, z)
        low = jnp.minimum(z, 0.0)
        high = z - low
        w = jnp.exp2(low - high)
        p = jnp.exp2(low) * (1.0 / (1.0 + w))
        if diagonal:
            p = jnp.where(eye, -p, p)
        acc[0, :, 0:tn] += fold(high)
        acc[1, :, 0:tn] += fold(p)
        acc[2, :, 0:tn] += fold(p * s)
        ws = [w[8 * i:8 * i + 8] for i in range(tm // 8)]
        while len(ws) > 1:
            odd = ws[-1:] if len(ws) % 2 else []
            ws = [ws[i] + (ws[i + 1] + ws[i] * ws[i + 1]) for i in range(0, len(ws) - 1, 2)] + odd
        x = ws[0]
        u = 1.0 + x
        acc[3, :, 0:tn] += jnp.log(u) + jnp.where(x < 1.0, x - (u - 1.0), 0.0) / u
        g[pl.ds(r0, tm), pl.ds(c0, tn)] = p.astype(BF16)

    def score(r0, c0, tm, tn):
        return dot(ie[pl.ds(r0, tm), :], te[pl.ds(c0, tn), :], NT)

    def tile(r0, c0, tm, tn, diagonal=False):
        entries(score(r0, c0, tm, tn), r0, c0, diagonal)

    def tiles(n, tm, tn, at, first=0):
        a, b = s0.at[0:tm, 0:tn], s1.at[0:tm, 0:tn]

        def place(t):
            r, c = at(t)
            return pl.multiple_of(r, h), pl.multiple_of(c, h)

        def scores(t, dst):
            dst[:] = score(*place(t), tm, tn)

        scores(first, a)

        def pair(i, _):
            t = first + 2 * i
            scores(t + 1, b)
            entries(a[:], *place(t))
            scores(jnp.minimum(t + 2, first + n - 1), a)
            entries(b[:], *place(t + 1))
            return 0

        lax.fori_loop(0, n // 2, pair, 0)

    pl.semaphore_wait(barrier, 7)
    ag_start(0)
    tx_copy(0).start()
    ag_start(1)
    tx_copy(1).start()

    ag_wait(0)
    ag_start(2)
    tx_copy(2).start()
    tile(0, 0, 4 * h, 4 * h, True)
    tx_copy(0).wait_recv()
    tx_copy(2).wait_recv()
    tile(0, 4 * h, 4 * h, 4 * h)

    ag_wait(1)
    ag_start(3)
    tx_copy(3).start()
    tile(4 * h, 8 * h, 4 * h, 4 * h, True)
    tx_copy(1).wait_recv()
    tx_copy(3).wait_recv()
    tile(4 * h, 12 * h, 4 * h, 4 * h)
    tiles(4, 4 * h, 4 * h, lambda t: (t // 2 * 4 * h, (1 - t // 2) * 8 * h + t % 2 * 4 * h))

    ag_wait(2)
    ag_start(4)
    tx_copy(4).start()
    tx_copy(4).wait_recv()
    tiles(6, 4 * h, 2 * h, lambda t: (t % 2 * 4 * h, 16 * h + t // 2 * 2 * h))

    ag_wait(3)
    ag_start(5)
    tx_copy(5).start()
    tiles(8, 6 * h, 2 * h, lambda t: (8 * h, t * 2 * h))
    ag_wait(4, 5)
    tx_copy(6).start()
    tx_copy(5).wait_recv()
    tiles(6, 6 * h, 2 * h, lambda t: (8 * h, t * 2 * h), 8)
    tiles(6, 4 * h, 2 * h, lambda t: (t % 2 * 4 * h, 22 * h + t // 2 * 2 * h))
    tx_copy(6).wait_recv()
    tiles(4, 7 * h, 2 * h, lambda t: (t % 2 * 7 * h, 28 * h + t // 2 * 2 * h))
    tiles(8, 2 * h, 4 * h, lambda t: (14 * h, t * 4 * h))

    near_of = {1: 0, 2: 1, 4: 2}

    def rs_copy(kind, m, dim, src, dst, n):
        return copy_to(sbuf.at[kind, src:src + n], rbuf.at[kind, dst:dst + n],
                       rs_send.at[kind, m], rs_recv.at[kind, m], nbr[kind][dim])

    def r1(s, hh):
        return (2 + near_of[s] * 2 + hh) * h

    rs = [(dim, irow(7, hh) + parts[dim][0], hh * h + parts[dim][0], parts[dim][1]) for hh in BOTH for dim in DIMS]
    rs += [(dim, irow(t, hh), r1(s, hh), h) for hh, dim, s, t in ways]
    rs += [(dim, irow(1 << dim, hh), (8 + dim * 2 + hh) * h, h) for hh in BOTH for dim in DIMS]

    def rs_do(kind, lo, hi, what):
        for m in range(lo, hi):
            getattr(rs_copy(kind, m, *rs[m]), what)()

    groups = [(*digits("esu"), [(7, 0), (7, 1)], digits("06"), None)]
    groups += [(*digits(w), [(s, hh) for s in LATE], digits(v[:2]), digits(v[2:]))
               for hh, w, v in ((0, "8gj", "6903"), (1, "bmp", "9c36"))]
    groups += [(*digits(w), [(s, hh) for s in EARLY], digits(v[:2]), digits(v[2:]))
               for hh, w, v in ((0, "004", "cf69"), (1, "48c", "fi9c"))]
    nstep = min(256, width)

    def settle(kind, blocks, sends, needs, add=None):
        if needs is not None:
            rs_do(kind, *needs, "wait_recv")
        for i, (s, hh) in enumerate(blocks):
            at = irow(s, hh)

            def total(lo, n, extra, i=i):
                v = tmp[i * h + lo:i * h + lo + n, :]
                if add is not None:
                    v = v + add[i * h + lo:i * h + lo + n, :]
                if extra is not None:
                    v = v + rbuf[kind, extra:extra + n, :].astype(F32)
                return v

            if s == 0:
                fin[kind, hh * h:(hh + 1) * h, :] = total(0, h, None)
            elif s in near_of:
                sbuf[kind, at:at + h, :] = total(0, h, r1(s, hh)).astype(BF16)
            elif s == 7:
                sbuf[kind, at:at + h, :] = total(0, h, None).astype(BF16)
            else:
                with_extra = {6: 0, 5: 1, 3: 2}[s]
                for k, (lo, n) in enumerate(parts):
                    extra = hh * h + lo if k == with_extra else None
                    sbuf[kind, at + lo:at + lo + n, :] = total(lo, n, extra).astype(BF16)
        rs_do(kind, *sends, "start")

    def dt_copy(i, n):
        return copy_to(far.at[0:n], near.at[0:n], dt_send.at[i], dt_recv.at[i], other)

    for q, (ri, own, par, blocks, sends, needs) in enumerate(groups):
        n = len(blocks) * h
        if q > 0:
            pl.semaphore_wait(credit.at[q - 1], 1)
            dt_copy(q - 1, len(groups[q - 1][3]) * h).wait_send()

        def d_txt(j, dst, c0, n=n):
            cols = pl.ds(pl.multiple_of(j * nstep, nstep), nstep)
            dst[0:n, cols] = dot(g[:, c0 * h:c0 * h + n], ie[:, cols], TN)

        def d_img(j, n=n, ri=ri):
            cols = pl.ds(pl.multiple_of(j * nstep, nstep), nstep)
            tmp[0:n, cols] = dot(g[ri * h:ri * h + n, :], te[:, cols], NN)

        def loop(f):
            lax.fori_loop(0, width // nstep, lambda j, _: (f(j), 0)[1], 0)

        loop(functools.partial(d_txt, dst=far, c0=par))
        dt_copy(q, n).start()
        loop(d_img)
        settle(0, blocks, sends, needs)
        loop(functools.partial(d_txt, dst=tmp, c0=own))
        dt_copy(q, n).wait_recv()
        settle(1, blocks, sends, needs, near)
        if q + 1 < len(groups):
            pl.semaphore_signal(credit.at[q], inc=1, device_id=other, device_id_type=MESH)

    sums[:] = jnp.zeros_like(sums)
    loss = LN2 * acc[0] + acc[3]
    for i, v in enumerate((loss, acc[2], acc[1])):
        v = jnp.sum(v, axis=0, keepdims=True)
        total = v[:, 0:128]
        for j in range(1, v.shape[1] // 128):
            total = total + v[:, j * 128:(j + 1) * 128]
        sums[i:i + 1, :] = total

    for kind, out in ((0, du_img), (1, du_txt)):
        for hh in BOTH:
            for dim in DIMS:
                m = 12 + hh * 3 + dim
                rs_copy(kind, m, *rs[m]).wait_recv()
            d = fin[kind, hh * h:(hh + 1) * h, :]
            for dim in DIMS:
                at = (8 + dim * 2 + hh) * h
                d = d + rbuf[kind, at:at + h, :].astype(F32)
            d = d * sc[2]
            u = raw[kind, hh * h:(hh + 1) * h, :]
            r = lax.rsqrt(jnp.sum(u * u, axis=1, keepdims=True))
            u = u * r
            along = jnp.sum(d * u, axis=1, keepdims=True)
            out[hh * h:(hh + 1) * h, :] = (r * (d - u * along)).astype(BF16)

    for kind in BOTH:
        for m in range(len(ag)):
            ag_copy(kind, m).wait_send()
        rs_do(kind, 0, len(rs), "wait_send")
    for i in range(len(share)):
        tx_copy(i).wait_send()
    dt_copy(len(groups) - 1, len(groups[-1][3]) * h).wait_send()


def scores_and_grads(sc, img_x, txt_x, w_img, w_txt):
    rows, width = img_x.shape
    h = rows // 2
    any_spec = pl.BlockSpec(memory_space=pl.ANY)
    vmem = pl.BlockSpec(memory_space=pltpu.VMEM)
    dma = pltpu.SemaphoreType.DMA
    copies = dma((2, 18))
    group = pltpu.VMEM((4 * h, width), F32)
    square = pltpu.VMEM((7 * h, 4 * h), F32)

    def block(n, w=width):
        return pltpu.VMEM((n * h, w), BF16)

    def both(*shape, dtype=BF16):
        return pltpu.VMEM((2, *shape), dtype)

    return pl.pallas_call(
        functools.partial(score_kernel, rows, width),
        out_shape=(jax.ShapeDtypeStruct((rows, width), BF16), jax.ShapeDtypeStruct((rows, width), BF16),
                   jax.ShapeDtypeStruct((8, 128), F32)),
        in_specs=[pl.BlockSpec(memory_space=pltpu.SMEM)] + [any_spec] * 4,
        out_specs=(vmem, vmem, vmem),
        scratch_shapes=[
            both(rows, width, dtype=F32), both(rows, width), block(16), block(32), block(16, 32 * h),
            both(16 * h, width), both(14 * h, width),
            group, group, group, square, square, both(rows, width, dtype=F32),
            pltpu.VMEM((4, 8, 4 * h), F32),
            dma((4,)), copies, copies, dma((7,)), dma((7,)), copies, copies,
            dma((5,)), dma((5,)), pltpu.SemaphoreType.REGULAR((4,)),
        ],
        compiler_params=pltpu.CompilerParams(collective_id=0, has_side_effects=True,
                                             vmem_limit_bytes=VMEM_BYTES),
        name="scores",
    )(sc, img_x, txt_x, w_img, w_txt)


def colours_of(width):
    n = width // 128
    a = -(-n // 3)
    b = -(-(n - a) // 2)
    return [(0, a * 128), (a * 128, b * 128), ((a + b) * 128, (n - a - b) * 128)]


def weight_kernel(rows, width, x_img, x_txt, du_img, du_txt, part, dw_img, dw_txt, total,
                  xm, um, mine, theirs, r1, r2, sbuf, sr,
                  load_sem, load_send, load_recv, s_send, s_recv, a_send, a_recv, b_send, b_recv,
                  c_send, c_recv, d_send, d_recv, e_send, e_recv, out_sem, free_sem):
    chip, core = position()
    other = device(chip, 1 - core)
    kinds = (core, 1 - core)
    nbr = [[neighbour(chip, core, dim, k) for dim in DIMS] for k in kinds]
    top = [lax.div(lax.rem(c + 1 - core, 4), 2) for c in chip]
    low = [lax.rem(c + 1 - core, 2) for c in chip]
    colours = colours_of(width)
    big = width // 8
    small = width // 64

    def pick(bits, s):
        return sum((lax.rem(b + (s >> i & 1), 2) << i for i, b in enumerate(bits)), 0)

    barrier = pltpu.get_barrier_semaphore()
    for dev in (*nbr[0], *nbr[1], other):
        pl.semaphore_signal(barrier, inc=1, device_id=dev, device_id_type=MESH)

    x_refs, du_refs = (x_img, x_txt), (du_img, du_txt)

    def for_core(f):
        for c in BOTH:
            @pl.when(core == c)
            def _(c=c):
                f(c)

    def own_loads(c):
        return (pltpu.make_async_copy(x_refs[c], xm.at[0:rows], load_sem.at[0]),
                pltpu.make_async_copy(du_refs[c], um.at[0:rows], load_sem.at[1]))

    def give(c):
        return (copy_to(x_refs[1 - c], xm.at[rows:2 * rows], load_send.at[0], load_recv.at[0], other),
                copy_to(du_refs[1 - c], um.at[rows:2 * rows], load_send.at[1], load_recv.at[1], other))

    sbuf[0] = part[:]
    for_core(lambda c: [cp.start() for cp in own_loads(c)])
    pl.semaphore_wait(barrier, 7)
    for_core(lambda c: [cp.start() for cp in give(c)])

    def scalar_copy(i):
        dev = other if i == 0 else nbr[(i - 1) // 3][(i - 1) % 3]
        return copy_to(sbuf.at[i], sr.at[i], s_send.at[i], s_recv.at[i], dev)

    def scalar_step(i):
        scalar_copy(i).wait_recv()
        sbuf[i + 1] = sbuf[i] + sr[i]

    scalar_copy(0).start()
    for cp in own_loads(0):
        cp.wait()
    for cp in give(0):
        cp.wait_recv()

    step = min(256, width)

    def weights(j, _):
        cols = pl.ds(pl.multiple_of(j * step, step), step)
        v = dot(xm[:], um[:, cols], TN)
        mine[:, :, cols] = v.reshape(8, big, step)
        return 0

    lax.fori_loop(0, width // step, weights, 0)
    scalar_step(0)

    def scatter_plan():
        plan = []
        for stage in DIMS:
            for c in DIMS:
                dims = [c, (c + 1) % 3, (c + 2) % 3]
                d = dims[2 - stage]
                gone = sum(1 << e for e in dims[3 - stage:])
                for s in range(8):
                    if s >> d & 1 and not s & gone:
                        plan.append((stage, c, d, s))
        return plan

    plan = scatter_plan()

    def slots(stage, c):
        return [(i, p) for i, p in enumerate(plan) if p[0] == stage and p[1] == c]

    home = pick(top, 0)

    def view(level, s, c):
        lo, n = colours[c]
        if level == 0:
            return mine.at[pick(top, s), :, lo:lo + n]
        return mine.at[home, pl.ds(pl.multiple_of(pick(low, s) * small, small), small), lo:lo + n]

    def landing(level, i, c):
        lo, n = colours[c]
        r = r1 if level == 0 else r2
        return r.at[[k for k, p in enumerate(plan) if p[1] == c].index(i), :, lo:lo + n]

    def scatter_copy(level, i):
        stage, c, d, s = plan[i]
        sems = (a_send, a_recv) if level == 0 else (b_send, b_recv)
        return copy_to(view(level, s, c), landing(level, i, c), sems[0].at[i], sems[1].at[i], nbr[level][d])

    def gather_copy(level, i):
        stage, c, d, s = plan[i]
        sems = (d_send, d_recv) if level == 0 else (c_send, c_recv)
        ref = view(level, s ^ (1 << d), c)
        return copy_to(ref, ref, sems[0].at[i], sems[1].at[i], nbr[level][d])

    def gather_arrival(level, i):
        stage, c, d, s = plan[i]
        sems = (d_send, d_recv) if level == 0 else (c_send, c_recv)
        ref = view(level, s, c)
        return copy_to(ref, ref, sems[0].at[i], sems[1].at[i], nbr[level][d])

    for level in BOTH:
        for stage in DIMS:
            k = 1 + level * 3 + stage
            scalar_copy(k).start()
            for c in DIMS:
                for i, _ in slots(stage, c):
                    scatter_copy(level, i).start()
            for c in DIMS:
                for i, (_, _, d, s) in slots(stage, c):
                    scatter_copy(level, i).wait_recv()
                    v = view(level, s ^ (1 << d), c)
                    v[:] = v[:] + landing(level, i, c)[:]
            scalar_step(k)
            for c in DIMS:
                for i, _ in slots(stage, c):
                    scatter_copy(level, i).wait_send()
        for dev in nbr[level]:
            pl.semaphore_signal(free_sem.at[level], inc=1, device_id=dev, device_id_type=MESH)
    total[:] = sbuf[7]

    def hand_copy(i, s, c):
        lo, n = colours[c]
        b = pick(top, s)
        return copy_to(mine.at[b, :, lo:lo + n], theirs.at[b, :, lo:lo + n], e_send.at[i], e_recv.at[i], other)

    pl.semaphore_wait(free_sem.at[1], 3)
    for stage in (2, 1, 0):
        for c in DIMS:
            for i, _ in slots(stage, c):
                gather_copy(1, i).start()
        for c in DIMS:
            for i, _ in slots(stage, c):
                gather_arrival(1, i).wait_recv()
    hands = []
    pl.semaphore_wait(free_sem.at[0], 3)
    for stage in (2, 1, 0):
        for c in DIMS:
            for i, _ in slots(stage, c):
                gather_copy(0, i).start()
        if stage == 2:
            for c in DIMS:
                hands.append((len(hands), 0, c))
                hand_copy(*hands[-1]).start()
        for c in DIMS:
            for i, (_, _, d, s) in slots(stage, c):
                gather_arrival(0, i).wait_recv()
                hands.append((len(hands), s, c))
                hand_copy(*hands[-1]).start()

    def outs(c):
        refs = (dw_img, dw_txt)
        return (pltpu.make_async_copy(mine, refs[c], out_sem.at[0]),
                pltpu.make_async_copy(theirs, refs[1 - c], out_sem.at[1]))

    for_core(lambda c: outs(c)[0].start())
    for hand in hands:
        hand_copy(*hand).wait_recv()
    for_core(lambda c: outs(c)[1].start())
    for cp in outs(0):
        cp.wait()
    for cp in give(0):
        cp.wait_send()
    for i in range(7):
        scalar_copy(i).wait_send()
    for level in BOTH:
        for i in range(len(plan)):
            gather_copy(level, i).wait_send()
    for hand in hands:
        hand_copy(*hand).wait_send()


def weight_grads(img_x, txt_x, du_img, du_txt, part):
    rows, width = img_x.shape
    any_spec = pl.BlockSpec(memory_space=pl.ANY)
    vmem = pl.BlockSpec(memory_space=pltpu.VMEM)
    dma = pltpu.SemaphoreType.DMA
    two = dma((2,))
    shape = (8, width // 8, width)
    pair = pltpu.VMEM((2 * rows, width), BF16)
    whole = pltpu.VMEM(shape, F32)
    dw_img, dw_txt, total = pl.pallas_call(
        functools.partial(weight_kernel, rows, width),
        out_shape=(jax.ShapeDtypeStruct(shape, F32), jax.ShapeDtypeStruct(shape, F32),
                   jax.ShapeDtypeStruct((8, 128), F32)),
        in_specs=[any_spec] * 4 + [vmem],
        out_specs=(any_spec, any_spec, vmem),
        scratch_shapes=[
            pair, pair, whole, whole,
            pltpu.VMEM((7, width // 8, width), F32),
            pltpu.VMEM((7, width // 64, width), F32),
            pltpu.VMEM((8, 8, 128), F32),
            pltpu.VMEM((7, 8, 128), F32),
            two, two, two, dma((7,)), dma((7,)), *[dma((21,))] * 8, dma((24,)), dma((24,)), two,
            pltpu.SemaphoreType.REGULAR((2,)),
        ],
        compiler_params=pltpu.CompilerParams(collective_id=1, has_side_effects=True, vmem_limit_bytes=VMEM_BYTES),
        name="weights",
    )(img_x, txt_x, du_img, du_txt, part)
    return dw_img.reshape(width, width), dw_txt.reshape(width, width), total


def solution(mesh):
    devices = mesh.shape["replica"] * mesh.shape["data"]
    batch = ("replica", "data")

    def local_fn(img_x, txt_x, w_img, w_txt, log_temp, logit_bias):
        total_rows = img_x.shape[0] * devices
        temp = jnp.exp(log_temp[0])
        sc = jnp.stack([temp * LOG2E, logit_bias[0] * LOG2E, temp / total_rows])
        du_img, du_txt, part = scores_and_grads(sc, img_x, txt_x, w_img, w_txt)
        dw_img, dw_txt, total = weight_grads(img_x, txt_x, du_img, du_txt, part)
        sums = jnp.sum(total, axis=1) / total_rows
        return sums[0:1], temp * sums[1:2], sums[2:3], dw_img, dw_txt

    spec = P(batch, None)
    return jax.shard_map(local_fn, mesh=mesh, in_specs=(spec, spec, P(), P(), P(), P()),
                         out_specs=(P(), P(), P(), P(), P()), check_vma=False)
```

time: 4050 us -> 229 us (0.06)
  waiting for transfers between devices: 2080 us -> 0 us
  matrix products: 1050 us -> 0 us
  loops' own time: 675 us -> 0 us
  Pallas kernels: 0 us -> 216 us
  local copies, waits for them, and re-layouts: 112 us -> 7.55 us
  blocking collectives: 79.9 us -> 0 us
    ppermute x255 -> x0, waiting for transfers between devices: 1990 us -> none  [the longest x127 1980 us: hop(): txt_blk = lax.ppermute(txt_blk, batch_axes, next_perm)]
    dot_general x388 -> x0, matrix products: 1050 us -> none  [the longest x128 408 us: tile_terms(): jnp.einsum('ij,id->jd', grad_b, img_emb, preferred_element_type=jnp.float32)]
    another operation x1 -> x0, loops' own time: 675 us -> none  [local_fn(): final_state = lax.fori_loop(1, dev_count, hop, init_state)]
    pallas_call x0 -> x2, Pallas kernels: none -> 216 us  [the longest x1 130 us: scores_and_grads(): pl.pallas_call(functools.partial(score_kernel, rows, width), out_shape=(j...]
    while x127 -> x0, local copies, waits for them, and re-layouts: 101 us -> none
    psum x1 -> x0, waiting for transfers between devices: 90.8 us -> none  [local_fn(): lax.psum((final_state[3], final_state[4], final_state[5], d_w_img, d_w_tx...]
    psum x1 -> x0, blocking collectives: 79.9 us -> none  [local_fn(): lax.psum((final_state[3], final_state[4], final_state[5], d_w_img, d_w_tx...]
  transfers between devices with their start and end apart: 256 -> 0, of which waited for: 131 -> 0; matrix products, arithmetic and copies ran while one was open for 18% -> 0% of each run, Pallas kernels for 0% -> 0%
where the time goes in v1:
time: 229 us
  Pallas kernels  216 us (94%)
  local copies, waits for them, and re-layouts  7.55 us (3%)
  between operations  3.78 us (2%)
    pallas_call x1, Pallas kernels, scores_and_grads(): pl.pallas_call(functools.partial(score_kernel, rows, width), out_shape=(j...  130 us
    pallas_call x1, Pallas kernels, weight_grads(): pl.pallas_call(functools.partial(weight_kernel, rows, width), out_shape=(...  86.7 us
    unnamed x4, local copies, waits for them, and re-layouts  6.96 us

profile of v1, /device:TPU:1, one launch (start us, length us, event | category | flops | bytes accessed | tf_op | source)
XLA Modules:
  0.0 229.1 jit_solution(18225938592365680418)
XLA Ops:
  2.0 0.6 pad_maximum_fusion.sc
  2.6 129.6 %scores.1 = (bf16[256,1024]{1,0:T(8,128)(2,1)}, bf16[256,1024]{1,0:T(8,128)(2,1)}, f32[8,128]{1,0:T(8,128)}) custom-call(f32[3]{0:T(128)} %pad_maximum_fusion.sc, bf16[256,1024]{1,0:T(8,128)(2,1)} %x_img.3, bf16[256,1024]{1,0:T(8,128)(2,1)} %x_txt.3, bf16[1024,1024]{1,0:T(8,128)(2,1)} %w_img.1, bf16[1024,1024]{1,0:T(8,128)(2,1)} %w_txt.1), custom_call_target="tpu_custom_call" | custom-call | tf_op jit(solution)/shard_map/scores/pallas_call | solution.py:374
  132.2 86.7 %weights.1 = (f32[8,128,1024]{2,1,0:T(8,128)}, f32[8,128,1024]{2,1,0:T(8,128)}, f32[8,128]{1,0:T(8,128)}) custom-call(bf16[256,1024]{1,0:T(8,128)(2,1)} %x_img.3, bf16[256,1024]{1,0:T(8,128)(2,1)} %x_txt.3, bf16[256,1024]{1,0:T(8,128)(2,1)} %get-tuple-element.11.du_img, bf16[256,1024]{1,0:T(8,128)(2,1)} %get-tuple-element.12.du_txt, ...), custom_call_target="tpu_custom_call" | custom-call | tf_op jit(solution)/shard_map/weights/pallas_call | solution.py:595
  218.9 0.8 reduce_sum.9
  219.7 0.6 fusion
  221.0 0.0 copy-start
  221.0 4.9 %copy.15 = f32[1024,1024]{1,0:T(8,128)} copy(f32[1024,1024]{1,0:T(8,128)} %bitcast.3) | data formatting | bytes 8388608
  225.9 0.0 copy-done
  225.9 2.0 copy.16
  (1 shorter events, 0.0 us)
Async XLA Ops:
  221.0 5.0 %copy-start = (f32[8,128,1024]{2,1,0:T(8,128)S(1)}, f32[8,128,1024]{2,1,0:T(8,128)}, u32[]{:S(2)}) copy-start(f32[8,128,1024]{2,1,0:T(8,128)} %get-tuple-element.16) | copy-start | bytes 12582916
